TPU v7x, 512 devices: a 4x2x32 block of a 4x8x32 slice. The times are simulated.
512 devices in a mesh: graphs: 2 (over y), rows: 32 (over z), cols: 4 (over x), sub: 2 (over core).
Axes of the slice: x: 4, y: 2, z: 32, core: 2. Of those that a mesh axis runs over, the one named last changes fastest.
The devices are a block of a 4x8x32 slice.
Arguments:
- current_block: float32 [16, 1048576], P(None, ('graphs', 'rows', 'cols', 'sub')), parts along dimension 1, may hold values from -1200 to 1200, as said below
- previous_block: float32 [16, 1048576], P(None, ('graphs', 'rows', 'cols', 'sub')), parts along dimension 1, may hold values from -1200 to 1200, as said below
- adjacency_tiles: float32 [24576, 128, 128], P(('graphs', 'rows', 'cols', 'sub')), parts along dimension 0, may hold values from -0.3125 to 0.3125
- tile_rows: int32 [24576], P(('graphs', 'rows', 'cols', 'sub')), parts along dimension 0, may hold values from 0 to 4095, as said below
- tile_cols: int32 [24576], P(('graphs', 'rows', 'cols', 'sub')), parts along dimension 0, may hold values from 0 to 4095, as said below
- tile_count: int32 [512], P(('graphs', 'rows', 'cols', 'sub')), parts along dimension 0, may hold values from 18 to 48, as said below
- locked: int32 [2], P('graphs'), parts along dimension 0, may hold values from 0 to 7
Outputs:
- w_basis: float32 [16, 1048576], P(None, ('graphs', 'rows', 'cols', 'sub')), parts along dimension 1
- w_image: float32 [16, 1048576], P(None, ('graphs', 'rows', 'cols', 'sub')), parts along dimension 1
- ritz_matrix: float32 [96, 48], P('graphs'), parts along dimension 0
There are 2 independent parts, one for each index of `graphs`. A program takes and returns all parts, laid end to end along the dimension named above; each array names one. Nothing has to cross between parts.
Inputs may be any that keep to these rules, and one draw needn't show every extreme that they name: `current_block`: entries of order one to some hundreds. `previous_block`: entries of order one to some hundreds. Slots d * 48 to (d + 1) * 48 - 1 belong to device d and name its own tile rows d * 16 to (d + 1) * 16 - 1. The first 16 slots of a device name its tile rows in order, with tile_cols equal to tile_rows. Slots past the device's count name tile row d * 16 and carry no weight. `tile_cols`: A slot of device d names a tile column from d * 16 - 8 to (d + 1) * 16 + 7. Slot 16 of a device names a tile of the block before it and slot 17 one of the block after it, where such a block exists. A pair of tile row and tile column may stand in several slots; their tiles add. `tile_count`: in every draw some device has all 48 slots live.
All inputs are finite; a program needn't handle non-finite values.
Results may differ from a plain program's by a relative error of at most 0.000094.
Values sent between devices are 32-bit elements; how exact they have to be, the bound alone decides.
A program may use at most 64 MiB of HBM per device.

v0:
```python
import jax
import jax.numpy as jnp
from jax import lax
from jax.sharding import PartitionSpec as P


def extended(value, sides, width):
    edges = {}
    for axis, dim in sides:
        devices, length = (lax.axis_size(axis), value.shape[dim])
        up = [(i, (i + 1) % devices) for i in range(devices - 1)]
        last = lax.slice_in_dim(value, length - width, length, axis=dim)
        initial = lax.slice_in_dim(value, 0, width, axis=dim)
        edges[dim] = (
            lax.ppermute(last, axis, up),
            lax.ppermute(initial, axis, [(b, a) for a, b in up]),
        )
    done = []
    for _, dim in sides:
        low, high = edges[dim]
        around = [(width, width) if d in done else (0, 0) for d in range(value.ndim)]
        value = jnp.concatenate([jnp.pad(low, around), value, jnp.pad(high, around)], axis=dim)
        done.append(dim)
    return value


def one_axis_at_a_time(value, axes):
    for axis in axes:
        value = lax.psum(value, axis)
    return value


def inner_products(left, right):
    return jnp.dot(left, right.T, precision=lax.Precision.HIGHEST)


def solve_lower(factor, values):
    return lax.linalg.triangular_solve(factor, values, left_side=True, lower=True)


def rayleigh_ritz(gram_b, gram_a):
    factor_b = jnp.linalg.cholesky(gram_b)
    symmetric = 0.5 * (gram_a + gram_a.T)
    halfway = solve_lower(factor_b, symmetric)
    return solve_lower(factor_b, halfway.T)


def operate(vectors, padded, adjacency_tiles, column_position, placing, span_tiles):
    channels, rows_here = vectors.shape
    tile_size = adjacency_tiles.shape[1]
    column_blocks = padded.reshape(channels, span_tiles, tile_size)
    gathered = jnp.take(column_blocks, column_position, axis=1)
    products = jnp.einsum(
        "cta,tab->ctb", gathered, adjacency_tiles, precision=lax.Precision.HIGHEST
    )
    summed = jnp.einsum("ctb,tr->crb", products, placing, precision=lax.Precision.HIGHEST)
    return vectors - summed.reshape(channels, rows_here)


def body(current_block, previous_block, adjacency_tiles, tile_rows, tile_cols, tile_count, locked):
    vectors_k, rows_here = current_block.shape
    tile_size = adjacency_tiles.shape[1]
    row_tiles = rows_here // tile_size
    slot_count = adjacency_tiles.shape[0]
    vertex_total = rows_here * lax.axis_size(("rows", "cols", "sub"))
    position = lax.axis_index(("rows", "cols", "sub"))
    reach_tiles = row_tiles // 2
    span_tiles = row_tiles + 2 * reach_tiles
    column_position = tile_cols - (position * row_tiles - reach_tiles)
    row_slot = tile_rows - position * row_tiles
    live_mask = (jnp.arange(slot_count, dtype=jnp.int32) < tile_count[0]).astype(jnp.float32)
    placing = (row_slot[:, None] == jnp.arange(row_tiles, dtype=jnp.int32)[None, :]).astype(
        jnp.float32
    )
    placing = placing * live_mask[:, None]
    stacked = jnp.concatenate([current_block, previous_block], axis=0)
    padded_pair = extended(stacked, ((("rows", "cols", "sub"), 1),), reach_tiles * tile_size)
    pair_image = operate(
        stacked, padded_pair, adjacency_tiles, column_position, placing, span_tiles
    )
    x_image = pair_image[:vectors_k]
    p_image = pair_image[vectors_k:]
    frozen_rows = jnp.arange(vectors_k, dtype=jnp.int32) < locked[0]
    frozen_diag = jnp.diag(frozen_rows.astype(jnp.float32))
    zero_rows = jnp.zeros((vectors_k,), jnp.float32)
    pad_diag = jnp.diag(jnp.concatenate([zero_rows, frozen_rows.astype(jnp.float32), zero_rows]))
    cross_sum, square_sum = (
        one_axis_at_a_time(jnp.sum(current_block * x_image, axis=1), ("rows", "cols", "sub")),
        one_axis_at_a_time(jnp.sum(current_block * current_block, axis=1), ("rows", "cols", "sub")),
    )
    quotient = cross_sum / (square_sum + 1e-06)
    residual = jnp.where(frozen_rows[:, None], 0.0, x_image - quotient[:, None] * current_block)
    gram_w = (
        one_axis_at_a_time(inner_products(residual, residual), ("rows", "cols", "sub"))
        / vertex_total
        + frozen_diag
    )
    factor = jnp.linalg.cholesky(gram_w)
    w_basis = solve_lower(factor, residual)
    padded = extended(w_basis, ((("rows", "cols", "sub"), 1),), reach_tiles * tile_size)
    w_image = operate(w_basis, padded, adjacency_tiles, column_position, placing, span_tiles)
    search = jnp.concatenate([current_block, w_basis, previous_block], axis=0)
    search_image = jnp.concatenate([x_image, w_image, p_image], axis=0)
    plain_sum, image_sum = (
        one_axis_at_a_time(inner_products(search, search), ("rows", "cols", "sub")),
        one_axis_at_a_time(inner_products(search, search_image), ("rows", "cols", "sub")),
    )
    gram_b = plain_sum / vertex_total + pad_diag
    gram_a = image_sum / vertex_total
    ritz_matrix = rayleigh_ritz(gram_b, gram_a)
    return (w_basis, w_image, ritz_matrix)


def solution(mesh):
    in_specs = (
        P(None, ("graphs", "rows", "cols", "sub")),
        P(None, ("graphs", "rows", "cols", "sub")),
        P(("graphs", "rows", "cols", "sub"), None, None),
        P(("graphs", "rows", "cols", "sub")),
        P(("graphs", "rows", "cols", "sub")),
        P(("graphs", "rows", "cols", "sub")),
        P("graphs"),
    )
    out_specs = (
        P(None, ("graphs", "rows", "cols", "sub")),
        P(None, ("graphs", "rows", "cols", "sub")),
        P("graphs", None),
    )
    return jax.shard_map(body, mesh=mesh, in_specs=in_specs, out_specs=out_specs, check_vma=False)
```

profile of v0, /device:TPU:33, one launch (start us, length us, event | category | flops | bytes accessed | tf_op | source)
XLA Modules:
  0.0 362.2 jit_solution(13121580219357382442)
XLA Ops:
  0.6 1.1 constant_dynamic-update-slice_fusion.1
  1.7 0.9 constant_dynamic-update-slice_fusion
  3.3 4.6 %collective-permute-start = (f32[32,1024]{1,0:T(8,128)}, f32[32,1024]{1,0:T(8,128)}, u32[]{:S(2)}, u32[]{:S(2)}) collective-permute-start(f32[32,1024]{1,0:T(8,128)} %get-tuple-element.22), channel_id=1, source_target_pairs={{0,1},{1,2},{2,3},{3,4},{4,5},{5,6},{6,7},{7,8},{8,9},{9,10},{10,1... | collective-permute-start | bytes 393224 | tf_op jit(solution)/shard_map/ppermute | solution.py:15
  7.9 40.7 %collective-permute-start.1 = (f32[32,1024]{1,0:T(8,128)S(1)}, f32[32,1024]{1,0:T(8,128)}, u32[]{:S(2)}, u32[]{:S(2)}) collective-permute-start(f32[32,1024]{1,0:T(8,128)S(1)} %get-tuple-element.23), channel_id=1, source_target_pairs={{1,0},{2,1},{3,2},{4,3},{5,4},{6,5},{7,6},{8,7},{9,8},{10,9},{11,1... | collective-permute-start | bytes 393224 | tf_op jit(solution)/shard_map/ppermute | solution.py:16
  52.5 1.8 copy_bitcast_fusion
  54.3 2.5 gather_fusion
  56.8 4.0 %fusion.2 = f32[48,32,128]{2,1,0:T(8,128)S(1)} fusion(f32[48,128,128]{2,1,0:T(8,128)S(1)} %copy-done, f32[48,32,128]{2,1,0:T(8,128)} %gather_fusion, pred[48]{0:T(512)(128)(4,1)S(1)} %get-tuple-element.18), kind=kOutput, calls=%fused_computation.5 | convolution fusion | flops 302186496 | bytes 4718640 | tf_op jit(solution)/shard_map/cta,tab->ctb/dot_general | solution.py:53
  60.8 0.9 fusion
  62.5 0.8 multiply_reduce_fusion
  63.3 43.8 %all-reduce.1 = (f32[16]{0:T(128)S(1)}, f32[16]{0:T(128)S(1)}) all-reduce(f32[16]{0:T(128)S(1)} %get-tuple-element.5, f32[16]{0:T(128)S(1)} %get-tuple-element.4), channel_id=1, replica_groups=mesh['graphs'=2,'rows'=32,'cols'=4,'sub'=2] {'rows'}, use_global_device_ids=true, to_apply=%region_1.2 | all-reduce | flops 32 | bytes 256 | tf_op jit(solution)/shard_map/psum | solution.py:29
  107.1 8.0 %all-reduce.3 = (f32[16]{0:T(128)S(1)}, f32[16]{0:T(128)S(1)}) all-reduce(f32[16]{0:T(128)S(1)} %get-tuple-element.8, f32[16]{0:T(128)S(1)} %get-tuple-element.9), channel_id=1, replica_groups=mesh['graphs'=2,'rows'=32,'cols'=4,'sub'=2] {'cols'}, use_global_device_ids=true, to_apply=%region_2.3 | all-reduce | flops 32 | bytes 256 | tf_op jit(solution)/shard_map/psum | solution.py:29
  115.2 19.1 %all-reduce.5 = (f32[16]{0:T(128)S(1)}, f32[16]{0:T(128)S(1)}) all-reduce(f32[16]{0:T(128)S(1)} %get-tuple-element.12, f32[16]{0:T(128)S(1)} %get-tuple-element.13), channel_id=1, replica_groups=mesh['graphs'=2,'rows'=32,'cols'=4,'sub'=2] {'sub'}, use_global_device_ids=true, to_apply=%region_3.4 | all-reduce | flops 32 | bytes 256 | tf_op jit(solution)/shard_map/psum | solution.py:29
  134.3 1.3 fusion.53
  135.6 40.0 %psum.111 = f32[16,16]{1,0:T(8,128)S(1)} all-reduce(f32[16,16]{1,0:T(8,128)S(1)} %fusion.53), channel_id=1, replica_groups=mesh['graphs'=2,'rows'=32,'cols'=4,'sub'=2] {'rows'}, use_global_device_ids=true, to_apply=%region_8.9 | all-reduce | flops 256 | bytes 2048 | tf_op jit(solution)/shard_map/psum | solution.py:29
  175.7 6.9 %psum.112 = f32[16,16]{1,0:T(8,128)S(1)} all-reduce(f32[16,16]{1,0:T(8,128)S(1)} %psum.111), channel_id=1, replica_groups=mesh['graphs'=2,'rows'=32,'cols'=4,'sub'=2] {'cols'}, use_global_device_ids=true, to_apply=%region_9.10 | all-reduce | flops 256 | bytes 2048 | tf_op jit(solution)/shard_map/psum | solution.py:29
  182.6 18.4 %psum.113 = f32[16,16]{1,0:T(8,128)S(1)} all-reduce(f32[16,16]{1,0:T(8,128)S(1)} %psum.112), channel_id=1, replica_groups=mesh['graphs'=2,'rows'=32,'cols'=4,'sub'=2] {'sub'}, use_global_device_ids=true, to_apply=%region_10.11 | all-reduce | flops 256 | bytes 2048 | tf_op jit(solution)/shard_map/psum | solution.py:29
  202.5 1.4 cholesky.31
  205.3 1.2 custom-call.12
  206.5 1.3 fusion.32
  207.9 2.9 collective-permute-start.2
  210.8 2.0 collective-permute-start.3
  212.8 2.0 fusion.20
  214.8 1.6 collective-permute-done.3
  217.1 2.3 gather_fusion.1
  219.4 3.8 %fusion.14 = f32[48,16,128]{2,1,0:T(8,128)S(1)} fusion(f32[48,128,128]{2,1,0:T(8,128)S(1)} %copy-done, f32[48,16,128]{2,1,0:T(8,128)} %gather_fusion.1, pred[48]{0:T(512)(128)(4,1)S(1)} %get-tuple-element.18), kind=kOutput, calls=%fused_computation.20 | convolution fusion | flops 151093248 | bytes 3932208 | tf_op jit(solution)/shard_map/cta,tab->ctb/dot_general | solution.py:53
  224.4 1.1 fusion.6
  225.5 78.5 %all-reduce = (f32[48,48]{0,1:T(8,128)S(1)}, f32[48,48]{0,1:T(8,128)S(1)}) all-reduce(f32[48,48]{0,1:T(8,128)} %fusion.6, f32[48,48]{0,1:T(8,128)} %fusion.20), channel_id=1, replica_groups=mesh['graphs'=2,'rows'=32,'cols'=4,'sub'=2] {'rows'}, use_global_device_ids=true, to_apply=%region_18.19 | all-reduce | flops 4608 | bytes 36864 | tf_op jit(solution)/shard_map/psum | solution.py:29
  304.0 14.9 %all-reduce.2 = (f32[48,48]{0,1:T(8,128)S(1)}, f32[48,48]{0,1:T(8,128)S(1)}) all-reduce(f32[48,48]{0,1:T(8,128)S(1)} %get-tuple-element.6, f32[48,48]{0,1:T(8,128)S(1)} %get-tuple-element.7), channel_id=1, replica_groups=mesh['graphs'=2,'rows'=32,'cols'=4,'sub'=2] {'cols'}, use_global_device_ids=true, to_apply=%region_19.20 | all-reduce | flops 4608 | bytes 36864 | tf_op jit(solution)/shard_map/psum | solution.py:29
  318.8 32.5 %all-reduce.4 = (f32[48,48]{0,1:T(8,128)S(1)}, f32[48,48]{0,1:T(8,128)S(1)}) all-reduce(f32[48,48]{0,1:T(8,128)S(1)} %get-tuple-element.10, f32[48,48]{0,1:T(8,128)S(1)} %get-tuple-element.11), channel_id=1, replica_groups=mesh['graphs'=2,'rows'=32,'cols'=4,'sub'=2] {'sub'}, use_global_device_ids=true, to_apply=%region_20.21 | all-reduce | flops 4608 | bytes 36864 | tf_op jit(solution)/shard_map/psum | solution.py:29
  351.7 4.4 %cholesky.65 = f32[48,48]{1,0:T(8,128)S(1)} custom-call(f32[48,48]{1,0:T(8,128)S(1)} %fusion.29), custom_call_target="Cholesky" | custom-call | tf_op jit(solution)/shard_map/jit(cholesky)/cholesky | solution.py:42
  357.4 3.7 %custom-call.15 = f32[1,48,48]{1,2,0:T(8,128)S(1)} custom-call(f32[1,48,48]{2,1,0:T(8,128)S(1)} %fusion.23), custom_call_target="InvertDiagBlocksLowerTriangular" | custom-call | tf_op jit(solution)/shard_map/triangular_solve/custom-call.3 | solution.py:38
  361.4 0.8 fusion.27
  (62 shorter events, 10.7 us)
Async XLA Ops:
  0.6 56.2 %copy-start = (f32[48,128,128]{2,1,0:T(8,128)S(1)}, f32[48,128,128]{2,1,0:T(8,128)}, u32[]{:S(2)}) copy-start(f32[48,128,128]{2,1,0:T(8,128)} %param.11) | copy-start | bytes 9437188
  3.3 49.1 %collective-permute-start = (f32[32,1024]{1,0:T(8,128)}, f32[32,1024]{1,0:T(8,128)}, u32[]{:S(2)}, u32[]{:S(2)}) collective-permute-start(f32[32,1024]{1,0:T(8,128)} %get-tuple-element.22), channel_id=1, source_target_pairs={{0,1},{1,2},{2,3},{3,4},{4,5},{5,6},{6,7},{7,8},{8,9},{9,10},{10,1... | collective-permute-start | bytes 393224 | tf_op jit(solution)/shard_map/ppermute | solution.py:15
  7.9 44.6 %collective-permute-start.1 = (f32[32,1024]{1,0:T(8,128)S(1)}, f32[32,1024]{1,0:T(8,128)}, u32[]{:S(2)}, u32[]{:S(2)}) collective-permute-start(f32[32,1024]{1,0:T(8,128)S(1)} %get-tuple-element.23), channel_id=1, source_target_pairs={{1,0},{2,1},{3,2},{4,3},{5,4},{6,5},{7,6},{8,7},{9,8},{10,9},{11,1... | collective-permute-start | bytes 393224 | tf_op jit(solution)/shard_map/ppermute | solution.py:16
  49.3 11.5 %copy-start.7 = (s32[48]{0:T(128)}, s32[48]{0:T(128)S(1)}, u32[]{:S(2)}) copy-start(s32[48]{0:T(128)S(1)} %broadcast_subtract_fusion) | copy-start | bytes 580
  50.0 10.8 %copy-start.9 = (f32[48]{0:T(128)}, f32[48]{0:T(128)S(1)}, u32[]{:S(2)}) copy-start(f32[48]{0:T(128)S(1)} %compare_convert_fusion) | copy-start | bytes 580
  51.1 1.3 copy-start.13
  56.8 5.7 %copy-start.2 = (f32[16,2048]{1,0:T(8,128)S(1)}, f32[16,2048]{1,0:T(8,128)}, u32[]{:S(2)}) copy-start(f32[16,2048]{1,0:T(8,128)} %param.9) | copy-start | bytes 393220
  61.8 0.7 copy-start.1
  134.3 70.4 %copy-start.12 = (f32[16]{0:T(128)}, f32[16]{0:T(128)S(1)}, u32[]{:S(2)}) copy-start(f32[16]{0:T(128)S(1)} %add_divide_fusion) | copy-start | bytes 196
  207.8 15.9 %copy-start.3 = (f32[16,2048]{1,0:T(8,128)}, f32[16,2048]{1,0:T(8,128)S(1)}, u32[]{:S(2)}) copy-start(f32[16,2048]{1,0:T(8,128)S(1)} %fusion.32) | copy-start | bytes 393220
  207.8 15.4 %copy-start.8 = (s32[48]{0:T(128)S(1)}, s32[48]{0:T(128)}, u32[]{:S(2)}) copy-start(s32[48]{0:T(128)} %copy-done.7) | copy-start | bytes 580
  207.8 15.4 %copy-start.10 = (f32[48]{0:T(128)S(1)}, f32[48]{0:T(128)}, u32[]{:S(2)}) copy-start(f32[48]{0:T(128)} %copy-done.9) | copy-start | bytes 580
  207.9 6.9 %collective-permute-start.2 = (f32[16,1024]{1,0:T(8,128)S(1)}, f32[16,1024]{1,0:T(8,128)S(1)}, u32[]{:S(2)}, u32[]{:S(2)}) collective-permute-start(f32[16,1024]{1,0:T(8,128)S(1)} %get-tuple-element.24), channel_id=1, source_target_pairs={{0,1},{1,2},{2,3},{3,4},{4,5},{5,6},{6,7},{7,8},{8,9},{9,10},{10,1... | collective-permute-start | bytes 196616 | tf_op jit(solution)/shard_map/ppermute | solution.py:15
  210.8 5.6 %collective-permute-start.3 = (f32[16,1024]{1,0:T(8,128)S(1)}, f32[16,1024]{1,0:T(8,128)S(1)}, u32[]{:S(2)}, u32[]{:S(2)}) collective-permute-start(f32[16,1024]{1,0:T(8,128)S(1)} %get-tuple-element.25), channel_id=1, source_target_pairs={{1,0},{2,1},{3,2},{4,3},{5,4},{6,5},{7,6},{8,7},{9,8},{10,9},{11,1... | collective-permute-start | bytes 196616 | tf_op jit(solution)/shard_map/ppermute | solution.py:16
  219.4 5.0 %copy-start.4 = (f32[16,2048]{1,0:T(8,128)S(1)}, f32[16,2048]{1,0:T(8,128)}, u32[]{:S(2)}) copy-start(f32[16,2048]{1,0:T(8,128)} %get-tuple-element.21) | copy-start | bytes 393220
  219.4 5.0 %copy-start.6 = (f32[16,2048]{1,0:T(8,128)S(1)}, f32[16,2048]{1,0:T(8,128)}, u32[]{:S(2)}) copy-start(f32[16,2048]{1,0:T(8,128)} %param.10) | copy-start | bytes 393220
  219.4 132.0 %copy-start.11 = (f32[48]{0:T(128)S(1)}, f32[48]{0:T(128)}, u32[]{:S(2)}) copy-start(f32[48]{0:T(128)} %pad_maximum_fusion.3) | copy-start | bytes 580
  223.7 0.7 copy-start.5
where the time goes:
time: 363 us; the launch traced here: 362 us
  blocking collectives  262 us (72%)
  starting transfers between devices  50.2 us (14%)
  other arithmetic  21 us (6%)
  matrix products  15.9 us (4%)
  local copies, waits for them, and re-layouts  9.13 us (3%)
    psum x9, blocking collectives, one_axis_at_a_time(): value = lax.psum(value, axis)  262 us
    ppermute x2, starting transfers between devices, extended(): lax.ppermute(initial, axis, [(b, a) for a, b in up])  42.7 us
    dot_general x2, matrix products, operate(): jnp.einsum('cta,tab->ctb', gathered, adjacency_tiles, precision=lax.Preci...  7.81 us
    ppermute x2, starting transfers between devices, extended(): lax.ppermute(last, axis, up)  7.51 us
  transfers between devices with their start and end apart: 4, of which 1 were waited for; matrix products, arithmetic and copies ran while one was open for 1% of the time, Pallas kernels for 0%

commit v1 on v0

--- a/solution.py
+++ b/solution.py
@@ -2,6 +2,11 @@
 import jax.numpy as jnp
 from jax import lax
 from jax.sharding import PartitionSpec as P
+
+
+def place_the_trails(along_axis, m):
+    res = lax.all_gather(m, along_axis).sum(axis=0)
+    return res
 
 
 def extended(value, sides, width):
@@ -26,7 +31,7 @@
 
 def one_axis_at_a_time(value, axes):
     for axis in axes:
-        value = lax.psum(value, axis)
+        value = place_the_trails(axis, value)
     return value
 
 

time: 363 us -> 404 us (1.11)
  blocking collectives: 262 us -> 292 us
  local copies, waits for them, and re-layouts: 9.13 us -> 15 us
  other arithmetic: 21 us -> 26.3 us
    psum x9 -> x0, blocking collectives: 262 us -> none  [one_axis_at_a_time(): value = lax.psum(value, axis)]
    all_gather x0 -> x9, blocking collectives: none -> 221 us  [place_the_trails(): res = lax.all_gather(m, along_axis).sum(axis=0)]
    unnamed x0 -> x3, blocking collectives: none -> 70.9 us
    unnamed x29 -> x44, local copies, waits for them, and re-layouts: 2.45 us -> 7.12 us
  transfers between devices with their start and end apart: 4 -> 4, of which waited for: 1 -> 0; matrix products, arithmetic and copies ran while one was open for 1% -> 3% of each run, Pallas kernels for 0% -> 0%
where the time goes in v1:
time: 404 us; the launch traced here: 403 us
  blocking collectives  292 us (72%)
  starting transfers between devices  49.9 us (12%)
  other arithmetic  26.3 us (7%)
  matrix products  16.2 us (4%)
  local copies, waits for them, and re-layouts  15 us (4%)
  between operations  4.1 us (1%)
    all_gather x9, blocking collectives, place_the_trails(): res = lax.all_gather(m, along_axis).sum(axis=0)  221 us
    unnamed x3, blocking collectives  70.9 us
    ppermute x2, starting transfers between devices, extended(): lax.ppermute(initial, axis, [(b, a) for a, b in up])  43.3 us
  transfers between devices with their start and end apart: 4, of which 0 were waited for; matrix products, arithmetic and copies ran while one was open for 3% of the time, Pallas kernels for 0%

profile of v1, /device:TPU:33, one launch (start us, length us, event | category | flops | bytes accessed | tf_op | source)
XLA Modules:
  0.0 403.1 jit_solution(12607340085229440633)
XLA Ops:
  3.3 4.6 %collective-permute-start = (f32[32,1024]{1,0:T(8,128)}, f32[32,1024]{1,0:T(8,128)}, u32[]{:S(2)}, u32[]{:S(2)}) collective-permute-start(f32[32,1024]{1,0:T(8,128)} %get-tuple-element.16), channel_id=1, source_target_pairs={{0,1},{1,2},{2,3},{3,4},{4,5},{5,6},{6,7},{7,8},{8,9},{9,10},{10,1... | collective-permute-start | bytes 393224 | tf_op jit(solution)/shard_map/ppermute | solution.py:20
  7.9 40.7 %collective-permute-start.1 = (f32[32,1024]{1,0:T(8,128)S(1)}, f32[32,1024]{1,0:T(8,128)}, u32[]{:S(2)}, u32[]{:S(2)}) collective-permute-start(f32[32,1024]{1,0:T(8,128)S(1)} %get-tuple-element.17), channel_id=1, source_target_pairs={{1,0},{2,1},{3,2},{4,3},{5,4},{6,5},{7,6},{8,7},{9,8},{10,9},{11,1... | collective-permute-start | bytes 393224 | tf_op jit(solution)/shard_map/ppermute | solution.py:21
  53.0 1.3 dynamic-slice
  54.2 1.3 dynamic-slice.1
  56.9 1.2 dynamic-slice.2
  59.3 1.8 copy_bitcast_fusion
  61.2 2.5 gather_fusion
  63.7 4.0 convolution_bitcast_fusion
  70.7 43.3 %all-reduce.6 = (f32[512]{0:T(512)S(1)}, f32[512]{0:T(512)S(1)}) all-reduce(f32[512]{0:T(512)S(1)} %dynamic-update-slice.6, f32[512]{0:T(512)S(1)} %dynamic-update-slice.9), channel_id=2, replica_groups=mesh['graphs'=2,'rows'=32,'cols'=4,'sub'=2] {'rows'}, use_global_device_ids=true, to_apply=%add | all-reduce | flops 1024 | bytes 8192
  114.7 8.1 %all-reduce.7 = (f32[64]{0:T(128)S(1)}, f32[64]{0:T(128)S(1)}) all-reduce(f32[64]{0:T(128)S(1)} %dynamic-update-slice.7, f32[64]{0:T(128)S(1)} %dynamic-update-slice.10), channel_id=3, replica_groups=mesh['graphs'=2,'rows'=32,'cols'=4,'sub'=2] {'cols'}, use_global_device_ids=true, to_apply=%add.1 | all-reduce | flops 128 | bytes 1024
  123.5 19.5 %all-reduce.8 = (f32[32]{0:T(128)S(1)}, f32[32]{0:T(128)S(1)}) all-reduce(f32[32]{0:T(128)S(1)} %dynamic-update-slice.8, f32[32]{0:T(128)S(1)} %dynamic-update-slice.11), channel_id=4, replica_groups=mesh['graphs'=2,'rows'=32,'cols'=4,'sub'=2] {'sub'}, use_global_device_ids=true, to_apply=%add.2 | all-reduce | flops 64 | bytes 512
  143.2 1.3 fusion.51
  144.5 38.8 %all-gather.6 = f32[512,16]{1,0:T(8,128)S(1)} all-gather(f32[16,16]{1,0:T(8,128)S(1)} %fusion.51), channel_id=8, replica_groups=mesh['graphs'=2,'rows'=32,'cols'=4,'sub'=2] {'rows'}, dimensions={0}, use_global_device_ids=true | all-gather | bytes 33792 | tf_op jit(solution)/shard_map/all_gather | solution.py:8
  183.3 9.1 %all-gather.7 = f32[64,16]{1,0:T(8,128)S(1)} all-gather(f32[16,16]{1,0:T(8,128)S(1)} %reduce_sum.163), channel_id=9, replica_groups=mesh['graphs'=2,'rows'=32,'cols'=4,'sub'=2] {'cols'}, dimensions={0}, use_global_device_ids=true | all-gather | bytes 5120 | tf_op jit(solution)/shard_map/all_gather | solution.py:8
  192.4 18.7 %all-gather.8 = f32[32,16]{1,0:T(8,128)S(1)} all-gather(f32[16,16]{1,0:T(8,128)S(1)} %reduce_sum.164), channel_id=10, replica_groups=mesh['graphs'=2,'rows'=32,'cols'=4,'sub'=2] {'sub'}, dimensions={0}, use_global_device_ids=true | all-gather | bytes 3072 | tf_op jit(solution)/shard_map/all_gather | solution.py:8
  212.0 1.4 cholesky.31
  216.1 1.3 fusion.29
  217.3 1.5 fusion.16
  219.5 49.2 %all-gather.9 = f32[1536,48]{1,0:T(8,128)} all-gather(f32[48,48]{1,0:T(8,128)S(1)} %fusion.16), channel_id=11, replica_groups=mesh['graphs'=2,'rows'=32,'cols'=4,'sub'=2] {'rows'}, dimensions={0}, use_global_device_ids=true | all-gather | bytes 304128 | tf_op jit(solution)/shard_map/all_gather | solution.py:8
  269.8 9.8 %all-gather.10 = f32[192,48]{1,0:T(8,128)S(1)} all-gather(f32[48,48]{1,0:T(8,128)S(1)} %reduce_sum.166), channel_id=12, replica_groups=mesh['graphs'=2,'rows'=32,'cols'=4,'sub'=2] {'cols'}, dimensions={0}, use_global_device_ids=true | all-gather | bytes 46080 | tf_op jit(solution)/shard_map/all_gather | solution.py:8
  279.6 17.7 %all-gather.11 = f32[96,48]{1,0:T(8,128)S(1)} all-gather(f32[48,48]{1,0:T(8,128)S(1)} %reduce_sum.167), channel_id=13, replica_groups=mesh['graphs'=2,'rows'=32,'cols'=4,'sub'=2] {'sub'}, dimensions={0}, use_global_device_ids=true | all-gather | bytes 27648 | tf_op jit(solution)/shard_map/all_gather | solution.py:8
  298.3 4.4 %cholesky.65 = f32[48,48]{1,0:T(8,128)S(1)} custom-call(f32[48,48]{1,0:T(8,128)S(1)} %fusion.26), custom_call_target="Cholesky" | custom-call | tf_op jit(solution)/shard_map/jit(cholesky)/cholesky | solution.py:47
  303.3 1.9 collective-permute-start.2
  305.3 2.6 collective-permute-start.3
  308.6 4.3 %custom-call.15 = f32[1,48,48]{1,2,0:T(8,128)} custom-call(f32[1,48,48]{2,1,0:T(8,128)S(1)} %fusion.19), custom_call_target="InvertDiagBlocksLowerTriangular" | custom-call | tf_op jit(solution)/shard_map/triangular_solve/custom-call.3 | solution.py:43
  312.9 1.6 copy_bitcast_fusion.1
  314.4 2.3 gather_fusion.1
  316.7 3.8 convolution_bitcast_fusion.1
  321.7 47.8 %all-gather.12 = f32[1536,48]{1,0:T(8,128)} all-gather(f32[48,48]{1,0:T(8,128)S(1)} %fusion.4), channel_id=14, replica_groups=mesh['graphs'=2,'rows'=32,'cols'=4,'sub'=2] {'rows'}, dimensions={0}, use_global_device_ids=true | all-gather | bytes 304128 | tf_op jit(solution)/shard_map/all_gather | solution.py:8
  370.7 10.8 %all-gather.13 = f32[192,48]{1,0:T(8,128)S(1)} all-gather(f32[48,48]{1,0:T(8,128)S(1)} %reduce_sum.169), channel_id=15, replica_groups=mesh['graphs'=2,'rows'=32,'cols'=4,'sub'=2] {'cols'}, dimensions={0}, use_global_device_ids=true | all-gather | bytes 46080 | tf_op jit(solution)/shard_map/all_gather | solution.py:8
  381.5 19.0 %all-gather.14 = f32[96,48]{1,0:T(8,128)S(1)} all-gather(f32[48,48]{1,0:T(8,128)S(1)} %reduce_sum.170), channel_id=16, replica_groups=mesh['graphs'=2,'rows'=32,'cols'=4,'sub'=2] {'sub'}, dimensions={0}, use_global_device_ids=true | all-gather | bytes 27648 | tf_op jit(solution)/shard_map/all_gather | solution.py:8
  401.6 1.6 fusion.23
  (101 shorter events, 22.0 us)
Async XLA Ops:
  0.6 63.1 %copy-start = (f32[48,128,128]{2,1,0:T(8,128)S(1)}, f32[48,128,128]{2,1,0:T(8,128)}, u32[]{:S(2)}) copy-start(f32[48,128,128]{2,1,0:T(8,128)} %param.11) | copy-start | bytes 9437188
  3.3 56.0 %collective-permute-start = (f32[32,1024]{1,0:T(8,128)}, f32[32,1024]{1,0:T(8,128)}, u32[]{:S(2)}, u32[]{:S(2)}) collective-permute-start(f32[32,1024]{1,0:T(8,128)} %get-tuple-element.16), channel_id=1, source_target_pairs={{0,1},{1,2},{2,3},{3,4},{4,5},{5,6},{6,7},{7,8},{8,9},{9,10},{10,1... | collective-permute-start | bytes 393224 | tf_op jit(solution)/shard_map/ppermute | solution.py:20
  7.9 51.4 %collective-permute-start.1 = (f32[32,1024]{1,0:T(8,128)S(1)}, f32[32,1024]{1,0:T(8,128)}, u32[]{:S(2)}, u32[]{:S(2)}) collective-permute-start(f32[32,1024]{1,0:T(8,128)S(1)} %get-tuple-element.17), channel_id=1, source_target_pairs={{1,0},{2,1},{3,2},{4,3},{5,4},{6,5},{7,6},{8,7},{9,8},{10,9},{11,1... | collective-permute-start | bytes 393224 | tf_op jit(solution)/shard_map/ppermute | solution.py:21
  49.3 18.4 %copy-start.8 = (s32[48]{0:T(128)}, s32[48]{0:T(128)S(1)}, u32[]{:S(2)}) copy-start(s32[48]{0:T(128)S(1)} %broadcast_subtract_fusion) | copy-start | bytes 580
  50.0 17.7 %copy-start.10 = (f32[48]{0:T(128)}, f32[48]{0:T(128)S(1)}, u32[]{:S(2)}) copy-start(f32[48]{0:T(128)S(1)} %compare_convert_fusion) | copy-start | bytes 580
  51.2 7.5 %copy-start.13 = (f32[16]{0:T(128)}, f32[16]{0:T(128)S(1)}, u32[]{:S(2)}) copy-start(f32[16]{0:T(128)S(1)} %fusion.50) | copy-start | bytes 196
  63.7 5.7 %copy-start.2 = (f32[16,2048]{1,0:T(8,128)S(1)}, f32[16,2048]{1,0:T(8,128)}, u32[]{:S(2)}) copy-start(f32[16,2048]{1,0:T(8,128)} %param.9) | copy-start | bytes 393220
  68.7 0.7 copy-start.1
  143.2 40.1 %copy-start.12 = (f32[16]{0:T(128)}, f32[16]{0:T(128)S(1)}, u32[]{:S(2)}) copy-start(f32[16]{0:T(128)S(1)} %add_divide_fusion) | copy-start | bytes 196
  217.3 103.7 %copy-start.3 = (f32[16,2048]{1,0:T(8,128)}, f32[16,2048]{1,0:T(8,128)S(1)}, u32[]{:S(2)}) copy-start(f32[16,2048]{1,0:T(8,128)S(1)} %fusion.29) | copy-start | bytes 393220
  269.8 50.7 %copy-start.9 = (s32[48]{0:T(128)S(1)}, s32[48]{0:T(128)}, u32[]{:S(2)}) copy-start(s32[48]{0:T(128)} %copy-done.8) | copy-start | bytes 580
  269.8 50.7 %copy-start.11 = (f32[48]{0:T(128)S(1)}, f32[48]{0:T(128)}, u32[]{:S(2)}) copy-start(f32[48]{0:T(128)} %copy-done.10) | copy-start | bytes 580
  303.3 9.5 %collective-permute-start.2 = (f32[16,1024]{1,0:T(8,128)}, f32[16,1024]{1,0:T(8,128)S(1)}, u32[]{:S(2)}, u32[]{:S(2)}) collective-permute-start(f32[16,1024]{1,0:T(8,128)} %get-tuple-element.18), channel_id=1, source_target_pairs={{0,1},{1,2},{2,3},{3,4},{4,5},{5,6},{6,7},{7,8},{8,9},{9,10},{10,1... | collective-permute-start | bytes 196616 | tf_op jit(solution)/shard_map/ppermute | solution.py:20
  305.3 7.6 %collective-permute-start.3 = (f32[16,1024]{1,0:T(8,128)}, f32[16,1024]{1,0:T(8,128)}, u32[]{:S(2)}, u32[]{:S(2)}) collective-permute-start(f32[16,1024]{1,0:T(8,128)} %get-tuple-element.19), channel_id=1, source_target_pairs={{1,0},{2,1},{3,2},{4,3},{5,4},{6,5},{7,6},{8,7},{9,8},{10,9},{11,1... | collective-permute-start | bytes 196616 | tf_op jit(solution)/shard_map/ppermute | solution.py:21
  316.7 4.4 %copy-start.4 = (f32[16,2048]{1,0:T(8,128)S(1)}, f32[16,2048]{1,0:T(8,128)}, u32[]{:S(2)}) copy-start(f32[16,2048]{1,0:T(8,128)} %get-tuple-element.14) | copy-start | bytes 393220
  316.7 4.4 %copy-start.5 = (f32[16,2048]{1,0:T(8,128)S(1)}, f32[16,2048]{1,0:T(8,128)}, u32[]{:S(2)}) copy-start(f32[16,2048]{1,0:T(8,128)} %get-tuple-element.15) | copy-start | bytes 393220
  316.7 4.4 %copy-start.7 = (f32[16,2048]{1,0:T(8,128)S(1)}, f32[16,2048]{1,0:T(8,128)}, u32[]{:S(2)}) copy-start(f32[16,2048]{1,0:T(8,128)} %param.10) | copy-start | bytes 393220
  321.1 0.7 copy-start.6
